TPU v7x, 32 devices: a whole 2x2x4 slice. The times are simulated.
32 devices in a mesh: grp: 16 (over z, y, core), seq: 2 (over x).
Axes of the slice: x: 2, y: 2, z: 4, core: 2. Of those that a mesh axis runs over, the one named last changes fastest.
Arguments:
- queries: bfloat16 [8192, 4096], P(('grp', 'seq')), may hold values from -8 to 8
- keys: bfloat16 [8192, 4096], P(('grp', 'seq')), may hold values from -6 to 6
- values: bfloat16 [8192, 4096], P(('grp', 'seq')), may hold values from -6 to 6
- global_pos: int32 [64], P(('grp', 'seq')), may hold values from 0 to 127
- layout: int32 [64, 32], P(('grp', 'seq')), may hold values from 0 to 63, all different within a row
Outputs:
- attended: bfloat16 [8192, 4096], P(('grp', 'seq'))
Inputs may be any that keep to these rules, and one draw needn't show every extreme that they name: `layout`: each row lists 32 different block indices, and every block is listed by some row.
All inputs are finite; a program needn't handle non-finite values.
Results may differ from a plain program's by a relative error of at most 0.0042.
Values may be sent and summed in bfloat16 or wider, within the bound.
A program may use at most 128 MiB of HBM per device.

v0:
```python
import math
import jax
import jax.numpy as jnp
from jax import lax
from jax.sharding import PartitionSpec as P

HEADS = 32
HEAD_DIM = 128
BLOCK = 128


def shifted(value, axis, by):
    count = lax.axis_size(axis)
    pairs = [(i, i + by) for i in range(count) if 0 <= i + by < count]
    return lax.ppermute(value, axis, pairs)


def pooled(source, blocks_dev):
    blocks = source.astype(jnp.float32).reshape(blocks_dev, BLOCK, HEADS, HEAD_DIM).mean(axis=1)
    spread = jnp.mean(blocks * blocks, axis=-1, keepdims=True)
    return (
        (blocks / jnp.sqrt(spread + 1e-06))
        .reshape(blocks_dev, HEADS * HEAD_DIM)
        .astype(jnp.bfloat16)
    )


def shards(queries, keys, values, global_pos, layout):
    rows_dev, model_width = queries.shape
    blocks_dev = rows_dev // BLOCK
    devices = lax.axis_size(("grp", "seq"))
    position = lax.axis_index(("grp", "seq"))
    score_scale = 1.0 / math.sqrt(HEAD_DIM)
    summary_keys = pooled(keys, blocks_dev)
    summary_values = pooled(values, blocks_dev)
    edge_last = jnp.stack([keys[rows_dev - BLOCK :], values[rows_dev - BLOCK :]])
    edge_first = jnp.stack([keys[:BLOCK], values[:BLOCK]])
    from_left = shifted(edge_last, ("grp", "seq"), 1)
    from_right = shifted(edge_first, ("grp", "seq"), -1)
    wide_keys = jnp.concatenate([from_left[0], keys, from_right[0]], axis=0)
    wide_values = jnp.concatenate([from_left[1], values, from_right[1]], axis=0)
    window_keys = jnp.stack(
        [wide_keys[block_at * BLOCK : (block_at + 3) * BLOCK] for block_at in range(blocks_dev)]
    )
    window_values = jnp.stack(
        [wide_values[block_at * BLOCK : (block_at + 3) * BLOCK] for block_at in range(blocks_dev)]
    )
    window_keys = window_keys.reshape(blocks_dev, 3 * BLOCK, HEADS, HEAD_DIM)
    window_values = window_values.reshape(blocks_dev, 3 * BLOCK, HEADS, HEAD_DIM)
    query_blocks = queries.reshape(blocks_dev, BLOCK, HEADS, HEAD_DIM)
    scores = (
        jnp.einsum("bqhd,bkhd->bhqk", query_blocks, window_keys, preferred_element_type=jnp.float32)
        * score_scale
    )
    key_block = (
        position * blocks_dev
        + jnp.arange(blocks_dev, dtype=jnp.int32)[:, None]
        + jnp.arange(3 * BLOCK, dtype=jnp.int32)[None, :] // BLOCK
        - 1
    )
    inside = (key_block >= 0) & (key_block < devices * blocks_dev)
    scores = jnp.where(inside[:, None, None, :], scores, -jnp.inf)
    peak = jnp.max(scores, axis=-1)
    weights = jnp.exp(scores - peak[..., None])
    totals = jnp.sum(weights, axis=-1)
    numerator = jnp.einsum(
        "bhqk,bkhd->bhqd",
        weights.astype(jnp.bfloat16),
        window_values,
        preferred_element_type=jnp.float32,
    )
    is_global = jnp.arange(BLOCK, dtype=jnp.int32)[None, :] == global_pos[:, None]
    group_keys, group_values = (
        lax.all_gather(summary_keys, "seq", axis=0, tiled=True),
        lax.all_gather(summary_values, "seq", axis=0, tiled=True),
    )
    piece_keys = lax.all_gather(group_keys, "grp", axis=0, tiled=True)
    piece_values = lax.all_gather(group_values, "grp", axis=0, tiled=True)
    length = piece_keys.shape[0]
    block_ids = jnp.arange(length, dtype=jnp.int32)
    listed = jnp.any(layout[:, :, None] == block_ids[None, None, :], axis=1)
    visible = listed[:, None, :] | is_global[:, :, None]
    part_scores = (
        jnp.einsum(
            "bqhd,jhd->bhqj",
            query_blocks,
            piece_keys.reshape(length, HEADS, HEAD_DIM),
            preferred_element_type=jnp.float32,
        )
        * score_scale
    )
    part_scores = jnp.where(visible[:, None, :, :], part_scores, -jnp.inf)
    new_peak = jnp.maximum(peak, jnp.max(part_scores, axis=-1))
    factor = jnp.exp(peak - new_peak)
    part_weights = jnp.exp(part_scores - new_peak[..., None])
    totals_next = totals * factor + jnp.sum(part_weights, axis=-1)
    numerator_next = numerator * factor[..., None] + jnp.einsum(
        "bhqj,jhd->bhqd",
        part_weights.astype(jnp.bfloat16),
        piece_values.reshape(length, HEADS, HEAD_DIM),
        preferred_element_type=jnp.float32,
    )
    result = numerator_next / totals_next[..., None]
    return jnp.transpose(result, (0, 2, 1, 3)).reshape(rows_dev, model_width).astype(jnp.bfloat16)


def solution(mesh):
    in_specs = (
        P(("grp", "seq"), None),
        P(("grp", "seq"), None),
        P(("grp", "seq"), None),
        P(("grp", "seq")),
        P(("grp", "seq"), None),
    )
    out_specs = P(("grp", "seq"), None)
    return jax.shard_map(shards, mesh=mesh, in_specs=in_specs, out_specs=out_specs, check_vma=False)
```

profile of v0, /device:TPU:0, one launch (start us, length us, event | category | flops | bytes accessed | tf_op | source)
XLA Modules:
  0.0 201.6 jit_solution(7318982374215686735)
XLA Ops:
  0.0 3.3 %copy.84 = bf16[256,4096]{0,1:T(8,128)(2,1)S(1)} copy(bf16[256,4096]{1,0:T(8,128)(2,1)} %param.6) | data formatting | bytes 4194304 | tf_op args[1]
  3.3 4.1 %copy.85 = bf16[256,4096]{0,1:T(8,128)(2,1)} copy(bf16[256,4096]{1,0:T(8,128)(2,1)} %param.7) | data formatting | bytes 4194304 | tf_op args[2]
  7.4 2.0 slice_bitcast_fusion.2
  9.3 0.0 copy-start
  9.4 1.6 pad_maximum_fusion.1
  10.9 1.3 collective-permute-start.1
  12.2 1.5 pad_maximum_fusion
  13.7 7.0 %collective-permute-start = (bf16[2,128,4096]{1,2,0:T(8,128)(2,1)}, bf16[2,128,4096]{1,2,0:T(8,128)(2,1)}, u32[]{:S(2)}, u32[]{:S(2)}) collective-permute-start(bf16[2,128,4096]{1,2,0:T(8,128)(2,1)} %pad_maximum_fusion), channel_id=1, source_target_pairs={{0,1},{1,2},{2,3},{3,4},{4,5},{5,6},{6,7},{7,8},{8,9},{9,10},{10,1... | collective-permute-start | bytes 6291464 | tf_op jit(solution)/shard_map/ppermute | solution.py:15
  20.7 0.5 convert_bitcast_fusion.1
  21.2 2.4 %convert_bitcast_fusion = f32[32,8,32,128]{3,1,2,0:T(8,128)} fusion(bf16[256,4096]{1,0:T(8,128)(2,1)S(1)} %copy-done.1), kind=kLoop, calls=%fused_computation.32 | loop fusion | flops 1048576 | bytes 6291456
  23.6 0.8 copy.116
  24.4 0.3 bitcast_reduce_fusion.2
  24.6 0.1 multiply_reduce_fusion.1
  24.7 0.1 divide_convert_fusion.1
  24.9 82.1 %all-gather = bf16[2,2,4096]{2,1,0:T(2,128)(2,1)S(1)} all-gather(bf16[1,2,4096]{2,1,0:T(2,128)(2,1)S(1)} %reshape.201), channel_id=1, replica_groups=mesh['grp'=16,'seq'=2] {'seq'}, dimensions={0}, use_global_device_ids=true | all-gather | bytes 49152 | tf_op jit(solution)/shard_map/all_gather | solution.py:74
  106.9 23.4 %all-gather.1 = bf16[16,4,4096]{2,1,0:T(4,128)(2,1)S(1)} all-gather(bf16[1,4,4096]{2,1,0:T(4,128)(2,1)S(1)} %reshape.203), channel_id=1, replica_groups=mesh['grp'=16,'seq'=2] {'grp'}, dimensions={0}, use_global_device_ids=true | all-gather | bytes 557056 | tf_op jit(solution)/shard_map/all_gather | solution.py:77
  130.3 2.9 %copy.117 = f32[32,8,32,128]{3,2,1,0:T(8,128)S(1)} copy(f32[32,8,32,128]{3,1,2,0:T(8,128)} %convert_bitcast_fusion) | data formatting | bytes 8388608
  133.3 0.3 bitcast_reduce_fusion.1
  133.5 0.1 multiply_reduce_fusion
  133.6 4.1 %copy.96 = bf16[1,256,32,128]{3,1,2,0:T(8,128)(2,1)} copy(bf16[1,256,32,128]{1,3,2,0:T(8,128)(2,1)} %bitcast.75) | data formatting | bytes 4194304 | tf_op jit(solution)/shard_map/concatenate | solution.py:41
  137.7 2.9 %copy.88 = bf16[1,256,32,128]{3,1,2,0:T(8,128)(2,1)} copy(bf16[1,256,32,128]{1,3,2,0:T(8,128)(2,1)S(1)} %bitcast.74) | data formatting | bytes 4194304 | tf_op jit(solution)/shard_map/concatenate | solution.py:40
  140.6 2.1 %copy.115 = bf16[32,8,32,128]{3,2,1,0:T(8,128)(2,1)S(1)} copy(bf16[32,8,32,128]{3,1,2,0:T(8,128)(2,1)} %bitcast.83) | data formatting | bytes 4194304
  142.7 1.5 reshape.193
  144.2 0.1 divide_convert_fusion
  144.3 4.4 %all-gather.2 = bf16[2,2,4096]{2,1,0:T(2,128)(2,1)S(1)} all-gather(bf16[1,2,4096]{2,1,0:T(2,128)(2,1)S(1)} %reshape.205), channel_id=1, replica_groups=mesh['grp'=16,'seq'=2] {'seq'}, dimensions={0}, use_global_device_ids=true | all-gather | bytes 49152 | tf_op jit(solution)/shard_map/all_gather | solution.py:75
  148.8 18.9 %all-gather.3 = bf16[16,4,4096]{2,1,0:T(4,128)(2,1)S(1)} all-gather(bf16[1,4,4096]{2,1,0:T(4,128)(2,1)S(1)} %reshape.207), channel_id=1, replica_groups=mesh['grp'=16,'seq'=2] {'grp'}, dimensions={0}, use_global_device_ids=true | all-gather | bytes 557056 | tf_op jit(solution)/shard_map/all_gather | solution.py:78
  167.7 0.5 reshape.196
  168.2 0.1 fusion.43
  168.4 0.1 iota_compare_fusion.1
  168.4 0.1 compare_and_fusion
  168.5 0.1 broadcast_or_fusion
  168.6 3.8 %fusion.54 = (f32[2,32,128]{2,0,1:T(2,128)S(1)}, f32[2,32,128,64]{2,3,0,1:T(8,128)}) fusion(bf16[2,128,32,128]{3,2,1,0:T(8,128)(2,1)S(1)} %bitcast.84, bf16[64,32,128,1]{2,1,0,3:T(8,128)(2,1)} %bitcast.86, pred[2,128,64]{1,2,0:T(8,128)(4,1)S(1)} %broadcast_or_fusion), kind=kOutput, calls=%fused_computation.83 | convolution fusion | flops 135782400 | bytes 4767744 | tf_op jit(solution)/shard_map/bqhd,jhd->bhqj/dot_general | solution.py:84
  172.4 1.7 fusion.53
  174.1 1.4 copy.98
  175.5 1.3 copy.92
  176.8 1.7 fusion.52
  178.5 1.3 copy.95
  179.8 0.7 copy.87
  180.5 5.2 %bitcast_reduce_fusion = (f32[2,32,128]{2,1,0:T(8,128)S(1)}, f32[2,32,384,128]{3,2,1,0:T(8,128)S(1)}) fusion(pred[2,384]{1,0:T(4,128)(4,1)S(1)} %compare_and_fusion, bf16[2,128,32,128]{3,2,1,0:T(8,128)(2,1)} %bitcast.85, bf16[1,128,32,128]{3,1,2,0:T(8,128)(2,1)} %copy.92, bf16[1,256,32,128]{3,1,2,0:T(8,128)(2,1)} %copy.88, ...), kind=kOutput, calls=%fused_computation.1 | convolution fusion | flops 839901184 | bytes 18907904 | tf_op jit(solution)/shard_map/bqhd,bkhd->bhqk/dot_general | solution.py:52
  185.6 4.0 %fusion.1 = f32[2,32,128]{2,1,0:T(8,128)S(1)} fusion(f32[2,32,384,128]{3,2,1,0:T(8,128)S(1)} %get-tuple-element.18, f32[2,32,128]{2,1,0:T(8,128)S(1)} %get-tuple-element.17, pred[2,384]{1,0:T(4,128)(4,1)S(1)} %compare_and_fusion), kind=kLoop, calls=%fused_computation.4 | loop fusion | flops 12574720 | bytes 12649216 | tf_op jit(solution)/shard_map/reduce_sum | solution.py:65
  189.7 0.6 fusion.33
  190.3 0.8 fusion.37
  191.1 0.2 copy-done.2
  191.3 0.3 copy-done.5
  191.5 0.3 copy-done.6
  191.9 6.1 %fusion.25 = bf16[2,128,32,128]{3,1,2,0:T(8,128)(2,1)S(1)} fusion(f32[32,128,2,128]{1,3,0,2:T(8,128)S(1)} %fusion.37, bf16[1,128,32,128]{3,1,2,0:T(8,128)(2,1)S(1)} %copy-done.5, bf16[1,256,32,128]{3,1,2,0:T(8,128)(2,1)S(1)} %copy-done.2, bf16[1,128,32,128]{3,1,2,0:T(8,128)(2,1)S(1)} %copy-done.6, f32[2,32,384,128]{3,2,1,0:T(8,128)S(1)} %get-tuple-element.18, ...), kind=kOutput, calls=%fused_computation.30 | convolution fusion | flops 847249408 | bytes 23167744 | tf_op jit(solution)/shard_map/bhqk,bkhd->bhqd/dot_general | solution.py:66
  197.9 1.4 copy.109
  199.3 2.3 %copy.144 = bf16[32,8,32,128]{3,1,2,0:T(8,128)(2,1)} copy(bf16[32,8,32,128]{3,2,1,0:T(8,128)(2,1)S(1)} %bitcast.78) | data formatting | bytes 4194304
  (27 shorter events, 0.2 us)
Async XLA Ops:
  9.3 11.4 %copy-start = (bf16[256,4096]{1,0:T(8,128)(2,1)S(1)}, bf16[256,4096]{1,0:T(8,128)(2,1)}, u32[]{:S(2)}) copy-start(bf16[256,4096]{1,0:T(8,128)(2,1)} %param.6) | copy-start | bytes 6291460
  10.9 161.5 %collective-permute-start.1 = (bf16[2,128,4096]{1,2,0:T(8,128)(2,1)}, bf16[2,128,4096]{1,2,0:T(8,128)(2,1)}, u32[]{:S(2)}, u32[]{:S(2)}) collective-permute-start(bf16[2,128,4096]{1,2,0:T(8,128)(2,1)} %pad_maximum_fusion.1), channel_id=1, source_target_pairs={{1,0},{2,1},{3,2},{4,3},{5,4},{6,5},{7,6},{8,7},{9,8},{10,9},{11,1... | collective-permute-start | bytes 6291464 | tf_op jit(solution)/shard_map/ppermute | solution.py:15
  13.7 7.5 %copy-start.1 = (bf16[256,4096]{1,0:T(8,128)(2,1)S(1)}, bf16[256,4096]{1,0:T(8,128)(2,1)}, u32[]{:S(2)}) copy-start(bf16[256,4096]{1,0:T(8,128)(2,1)} %param.7) | copy-start | bytes 6291460
  13.7 163.0 %collective-permute-start = (bf16[2,128,4096]{1,2,0:T(8,128)(2,1)}, bf16[2,128,4096]{1,2,0:T(8,128)(2,1)}, u32[]{:S(2)}, u32[]{:S(2)}) collective-permute-start(bf16[2,128,4096]{1,2,0:T(8,128)(2,1)} %pad_maximum_fusion), channel_id=1, source_target_pairs={{0,1},{1,2},{2,3},{3,4},{4,5},{5,6},{6,7},{7,8},{8,9},{9,10},{10,1... | collective-permute-start | bytes 6291464 | tf_op jit(solution)/shard_map/ppermute | solution.py:15
  140.6 27.6 %copy-start.7 = (s32[2,32]{1,0:T(2,128)S(1)}, s32[2,32]{1,0:T(2,128)}, u32[]{:S(2)}) copy-start(s32[2,32]{1,0:T(2,128)} %param.9) | copy-start | bytes 772
  140.6 27.7 %copy-start.8 = (s32[2]{0:T(128)S(1)}, s32[2]{0:T(128)}, u32[]{:S(2)}) copy-start(s32[2]{0:T(128)} %param.8) | copy-start | bytes 28
  142.7 29.7 %copy-start.3 = (bf16[32,8,32,128]{3,2,1,0:T(8,128)(2,1)}, bf16[32,8,32,128]{3,2,1,0:T(8,128)(2,1)S(1)}, u32[]{:S(2)}) copy-start(bf16[32,8,32,128]{3,2,1,0:T(8,128)(2,1)S(1)} %copy.115) | copy-start | bytes 6291460
  185.6 4.1 %copy-start.4 = (f32[2,32,128,64]{2,3,0,1:T(8,128)S(1)}, f32[2,32,128,64]{2,3,0,1:T(8,128)}, u32[]{:S(2)}) copy-start(f32[2,32,128,64]{2,3,0,1:T(8,128)} %get-tuple-element.20) | copy-start | bytes 6291460
  189.7 1.6 copy-start.2
  189.7 1.8 copy-start.5
  189.7 2.2 %copy-start.6 = (bf16[1,128,32,128]{3,1,2,0:T(8,128)(2,1)S(1)}, bf16[1,128,32,128]{3,1,2,0:T(8,128)(2,1)}, u32[]{:S(2)}) copy-start(bf16[1,128,32,128]{3,1,2,0:T(8,128)(2,1)} %copy.95) | copy-start | bytes 3145732
where the time goes:
time: 202 us
  blocking collectives  129 us (64%)
  local copies, waits for them, and re-layouts  36.7 us (18%)
  matrix products  15.8 us (8%)
  other arithmetic  11.8 us (6%)
  starting transfers between devices  8.25 us (4%)
    all_gather x1, blocking collectives, shards(): lax.all_gather(summary_keys, 'seq', axis=0, tiled=True)  82.1 us
    all_gather x1, blocking collectives, shards(): piece_keys = lax.all_gather(group_keys, 'grp', axis=0, tiled=True)  23.4 us
    all_gather x1, blocking collectives, shards(): piece_values = lax.all_gather(group_values, 'grp', axis=0, tiled=True)  18.9 us
    unnamed x28, local copies, waits for them, and re-layouts  16.3 us
    ppermute x2, starting transfers between devices, shifted(): return lax.ppermute(value, axis, pairs)  8.25 us
    concatenate x3, local copies, waits for them, and re-layouts, shards(): wide_values = jnp.concatenate([from_left[1], values, from_right[1]], axis=0)  6.82 us
    dot_general x1, matrix products, shards(): jnp.einsum('bhqk,bkhd->bhqd', weights.astype(jnp.bfloat16), window_values...  6.06 us
    dot_general x1, matrix products, shards(): jnp.einsum('bqhd,bkhd->bhqk', query_blocks, window_keys, preferred_elemen...  5.16 us
  transfers between devices with their start and end apart: 2, of which 0 were waited for; matrix products, arithmetic and copies ran while one was open for 14% of the time, Pallas kernels for 0%

commit v1 on v0

--- a/solution.py
+++ b/solution.py
@@ -74,8 +74,13 @@
         lax.all_gather(summary_keys, "seq", axis=0, tiled=True),
         lax.all_gather(summary_values, "seq", axis=0, tiled=True),
     )
-    piece_keys = lax.all_gather(group_keys, "grp", axis=0, tiled=True)
-    piece_values = lax.all_gather(group_values, "grp", axis=0, tiled=True)
+    piece_keys, piece_values = jnp.split(
+        lax.all_gather(
+            jnp.concatenate([group_keys, group_values], axis=1), "grp", axis=0, tiled=True
+        ),
+        [group_keys.shape[1]],
+        axis=1,
+    )
     length = piece_keys.shape[0]
     block_ids = jnp.arange(length, dtype=jnp.int32)
     listed = jnp.any(layout[:, :, None] == block_ids[None, None, :], axis=1)

time: 202 us -> 159 us (0.79)
  the two profiles are of different devices: /device:TPU:0 before, /device:TPU:1 now
where the time goes in v1:
time: 159 us; the launch traced here: 158 us
  waiting for transfers between devices  68.9 us (43%)
  local copies, waits for them, and re-layouts  33.9 us (21%)
  matrix products  14.5 us (9%)
  between operations  13.7 us (9%)
  other arithmetic  12 us (8%)
  starting transfers between devices  8.16 us (5%)
  blocking collectives  7.19 us (5%)
    ppermute x2, waiting for transfers between devices, shifted(): return lax.ppermute(value, axis, pairs)  47.7 us
    all_gather x1, waiting for transfers between devices, shards(): lax.all_gather(jnp.concatenate([group_keys, group_values], axis=1), 'grp'...  21.2 us
    unnamed x29, local copies, waits for them, and re-layouts  16.2 us
    ppermute x2, starting transfers between devices, shifted(): return lax.ppermute(value, axis, pairs)  8.16 us
    concatenate x3, local copies, waits for them, and re-layouts, shards(): wide_values = jnp.concatenate([from_left[1], values, from_right[1]], axis=0)  6.11 us
    dot_general x1, matrix products, shards(): jnp.einsum('bhqk,bkhd->bhqd', weights.astype(jnp.bfloat16), window_values...  6.06 us
    dot_general x1, matrix products, shards(): jnp.einsum('bqhd,bkhd->bhqk', query_blocks, window_keys, preferred_elemen...  4.9 us
    concatenate x3, local copies, waits for them, and re-layouts, shards(): wide_keys = jnp.concatenate([from_left[0], keys, from_right[0]], axis=0)  4.86 us
  transfers between devices with their start and end apart: 3, of which 3 were waited for; matrix products, arithmetic and copies ran while one was open for 19% of the time, Pallas kernels for 0%

profile of v1, /device:TPU:1, one launch (start us, length us, event | category | flops | bytes accessed | tf_op | source)
XLA Modules:
  0.0 158.4 jit_solution(4857567678383922906)
XLA Ops:
  6.5 2.1 %convert_bitcast_fusion.1 = f32[32,8,32,128]{3,1,2,0:T(8,128)S(1)} fusion(bf16[256,4096]{1,0:T(8,128)(2,1)} %param.6), kind=kLoop, calls=%fused_computation.33 | loop fusion | flops 1048576 | bytes 6291456
  8.6 0.8 copy.117
  9.4 0.3 bitcast_reduce_fusion.2
  9.7 0.1 multiply_reduce_fusion.1
  9.8 0.1 divide_convert_fusion.1
  9.9 3.9 %all-gather = bf16[2,2,4096]{2,1,0:T(2,128)(2,1)S(1)} all-gather(bf16[1,2,4096]{2,1,0:T(2,128)(2,1)S(1)} %reshape.201), channel_id=1, replica_groups=mesh['grp'=16,'seq'=2] {'seq'}, dimensions={0}, use_global_device_ids=true | all-gather | bytes 49152 | tf_op jit(solution)/shard_map/all_gather | solution.py:74
  13.8 0.5 convert_bitcast_fusion
  14.3 0.8 copy.118
  15.1 0.3 bitcast_reduce_fusion.1
  15.4 0.1 multiply_reduce_fusion
  15.5 0.1 divide_convert_fusion
  15.6 3.3 %all-gather.1 = bf16[2,2,4096]{2,1,0:T(2,128)(2,1)S(1)} all-gather(bf16[1,2,4096]{2,1,0:T(2,128)(2,1)S(1)} %reshape.203), channel_id=1, replica_groups=mesh['grp'=16,'seq'=2] {'seq'}, dimensions={0}, use_global_device_ids=true | all-gather | bytes 49152 | tf_op jit(solution)/shard_map/all_gather | solution.py:75
  18.8 0.7 maximum_bitcast_fusion
  19.5 3.3 %copy.84 = bf16[256,4096]{0,1:T(8,128)(2,1)S(1)} copy(bf16[256,4096]{1,0:T(8,128)(2,1)} %param.6) | data formatting | bytes 4194304 | tf_op args[1]
  22.8 4.1 %copy.85 = bf16[256,4096]{0,1:T(8,128)(2,1)} copy(bf16[256,4096]{1,0:T(8,128)(2,1)} %param.7) | data formatting | bytes 4194304 | tf_op args[2]
  26.9 2.0 %slice_bitcast_fusion.2 = (bf16[1,128,4096]{1,2,0:T(8,128)(2,1)S(1)}, bf16[1,128,4096]{1,2,0:T(8,128)(2,1)S(1)}, bf16[1,128,4096]{1,2,0:T(8,128)(2,1)S(1)}, bf16[1,128,4096]{1,2,0:T(8,128)(2,1)S(1)}) fusion(bf16[256,4096]{0,1:T(8,128)(2,1)} %copy.85, bf16[256,4096]{0,1:T(8,128)(2,1)S(1)} %copy.84), kind=kLoop, calls=%fused_computation.46 | loop fusion | bytes 8388608 | tf_op jit(solution)/shard_map/stack | solution.py:36
  28.9 1.5 pad_maximum_fusion.1
  30.4 6.3 %collective-permute-start.1 = (bf16[2,128,4096]{1,2,0:T(8,128)(2,1)}, bf16[2,128,4096]{1,2,0:T(8,128)(2,1)}, u32[]{:S(2)}, u32[]{:S(2)}) collective-permute-start(bf16[2,128,4096]{1,2,0:T(8,128)(2,1)} %pad_maximum_fusion.1), channel_id=1, source_target_pairs={{1,0},{2,1},{3,2},{4,3},{5,4},{6,5},{7,6},{8,7},{9,8},{10,9},{11,1... | collective-permute-start | bytes 6291464 | tf_op jit(solution)/shard_map/ppermute | solution.py:15
  36.6 1.5 pad_maximum_fusion
  38.1 1.9 %collective-permute-start = (bf16[2,128,4096]{1,2,0:T(8,128)(2,1)}, bf16[2,128,4096]{1,2,0:T(8,128)(2,1)}, u32[]{:S(2)}, u32[]{:S(2)}) collective-permute-start(bf16[2,128,4096]{1,2,0:T(8,128)(2,1)} %pad_maximum_fusion), channel_id=1, source_target_pairs={{0,1},{1,2},{2,3},{3,4},{4,5},{5,6},{6,7},{7,8},{8,9},{9,10},{10,1... | collective-permute-start | bytes 6291464 | tf_op jit(solution)/shard_map/ppermute | solution.py:15
  40.1 4.1 %copy.96 = bf16[1,256,32,128]{3,1,2,0:T(8,128)(2,1)} copy(bf16[1,256,32,128]{1,3,2,0:T(8,128)(2,1)} %bitcast.86) | data formatting | bytes 4194304 | tf_op jit(solution)/shard_map/concatenate | solution.py:41
  44.2 2.9 %copy.88 = bf16[1,256,32,128]{3,1,2,0:T(8,128)(2,1)} copy(bf16[1,256,32,128]{1,3,2,0:T(8,128)(2,1)S(1)} %bitcast.85) | data formatting | bytes 4194304 | tf_op jit(solution)/shard_map/concatenate | solution.py:40
  47.0 2.2 %copy.116 = bf16[32,8,32,128]{3,2,1,0:T(8,128)(2,1)S(1)} copy(bf16[32,8,32,128]{3,1,2,0:T(8,128)(2,1)} %bitcast.94) | data formatting | bytes 4194304
  49.3 0.1 fusion.42
  49.5 0.1 compare_and_fusion
  49.5 0.1 broadcast_or_fusion
  49.6 21.2 %all-gather.5.cloned.1.call-done = bf16[16,4,8192]{2,1,0:T(4,128)(2,1)} async-done(((bf16[1,4,8192]{2,1,0:T(4,128)(2,1)}), bf16[16,4,8192]{2,1,0:T(4,128)(2,1)}) %all-gather.5.cloned.1.call-update) | async-done | bytes 1048592 | tf_op jit(solution)/shard_map/all_gather | solution.py:78
  70.9 1.3 reshape.206
  72.2 0.9 slice_bitcast_fusion.4
  73.1 0.1 copy.119
  73.2 2.8 %fusion.53 = (f32[2,32,128]{2,0,1:T(2,128)S(1)}, f32[2,32,128,64]{2,3,0,1:T(8,128)}) fusion(bf16[2,128,32,128]{3,2,1,0:T(8,128)(2,1)S(1)} %bitcast.95, bf16[64,32,128,1]{2,1,0,3:T(8,128)(2,1)S(1)} %bitcast.97, pred[2,128,64]{1,2,0:T(8,128)(4,1)S(1)} %broadcast_or_fusion), kind=kOutput, calls=%fused_computation.86 | convolution fusion | flops 135782400 | bytes 4767744 | tf_op jit(solution)/shard_map/bqhd,jhd->bhqj/dot_general | solution.py:89
  76.0 28.0 %collective-permute-done.1 = bf16[2,128,4096]{1,2,0:T(8,128)(2,1)} collective-permute-done((bf16[2,128,4096]{1,2,0:T(8,128)(2,1)}, bf16[2,128,4096]{1,2,0:T(8,128)(2,1)}, u32[]{:S(2)}, u32[]{:S(2)}) %collective-permute-start.1) | collective-permute-done | bytes 2097184 | tf_op jit(solution)/shard_map/ppermute | solution.py:15
  104.0 1.7 %fusion.52 = (bf16[1,128,4096]{1,2,0:T(8,128)(2,1)S(1)}, bf16[1,128,4096]{1,2,0:T(8,128)(2,1)S(1)}) fusion(bf16[2,128,4096]{1,2,0:T(8,128)(2,1)} %collective-permute-done.1), kind=kLoop, calls=%fused_computation.85 | loop fusion | bytes 4194304 | tf_op jit(solution)/shard_map/slice | solution.py:41
  105.7 0.7 copy.98
  106.3 1.3 copy.92
  107.7 19.6 %collective-permute-done = bf16[2,128,4096]{1,2,0:T(8,128)(2,1)} collective-permute-done((bf16[2,128,4096]{1,2,0:T(8,128)(2,1)}, bf16[2,128,4096]{1,2,0:T(8,128)(2,1)}, u32[]{:S(2)}, u32[]{:S(2)}) %collective-permute-start) | collective-permute-done | bytes 2097184 | tf_op jit(solution)/shard_map/ppermute | solution.py:15
  127.3 1.7 %fusion.51 = (bf16[1,128,4096]{1,2,0:T(8,128)(2,1)S(1)}, bf16[1,128,4096]{1,2,0:T(8,128)(2,1)S(1)}) fusion(bf16[2,128,4096]{1,2,0:T(8,128)(2,1)} %collective-permute-done), kind=kLoop, calls=%fused_computation.84 | loop fusion | bytes 4194304 | tf_op jit(solution)/shard_map/slice | solution.py:41
  129.0 1.3 copy.95
  130.3 0.7 copy.87
  131.0 4.9 %bitcast_reduce_fusion = (f32[2,32,128]{2,1,0:T(8,128)S(1)}, f32[2,32,384,128]{3,2,1,0:T(8,128)S(1)}) fusion(pred[2,384]{1,0:T(4,128)(4,1)S(1)} %compare_and_fusion, bf16[2,128,32,128]{3,2,1,0:T(8,128)(2,1)} %bitcast.96, bf16[1,128,32,128]{3,1,2,0:T(8,128)(2,1)} %copy.92, bf16[1,256,32,128]{3,1,2,0:T(8,128)(2,1)} %copy.88, ...), kind=kOutput, calls=%fused_computation.1 | convolution fusion | flops 839901184 | bytes 18907904 | tf_op jit(solution)/shard_map/bqhd,bkhd->bhqk/dot_general | solution.py:52
  135.9 3.9 %fusion.1 = f32[2,32,128]{2,1,0:T(8,128)S(1)} fusion(f32[2,32,384,128]{3,2,1,0:T(8,128)S(1)} %get-tuple-element.20, f32[2,32,128]{2,1,0:T(8,128)S(1)} %get-tuple-element.19, pred[2,384]{1,0:T(4,128)(4,1)S(1)} %compare_and_fusion), kind=kLoop, calls=%fused_computation.4 | loop fusion | flops 12574720 | bytes 12649216 | tf_op jit(solution)/shard_map/reduce_sum | solution.py:65
  139.9 0.6 fusion.33
  140.6 0.8 fusion.37
  141.3 0.2 copy-done.1
  141.5 0.3 copy-done.5
  141.8 6.1 %fusion.25 = bf16[2,128,32,128]{3,1,2,0:T(8,128)(2,1)S(1)} fusion(f32[32,128,2,128]{1,3,0,2:T(8,128)S(1)} %fusion.37, bf16[1,128,32,128]{3,1,2,0:T(8,128)(2,1)S(1)} %copy.98, bf16[1,256,32,128]{3,1,2,0:T(8,128)(2,1)S(1)} %copy-done.1, bf16[1,128,32,128]{3,1,2,0:T(8,128)(2,1)S(1)} %copy-done.5, f32[2,32,384,128]{3,2,1,0:T(8,128)S(1)} %get-tuple-element.20, ...), kind=kOutput, calls=%fused_computation.30 | convolution fusion | flops 847249408 | bytes 23167744 | tf_op jit(solution)/shard_map/bhqk,bkhd->bhqd/dot_general | solution.py:66
  147.8 1.4 copy.109
  149.2 2.3 %copy.146 = bf16[32,8,32,128]{3,1,2,0:T(8,128)(2,1)} copy(bf16[32,8,32,128]{3,2,1,0:T(8,128)(2,1)S(1)} %bitcast.89) | data formatting | bytes 4194304
  (28 shorter events, 0.3 us)
Async XLA Ops:
  6.5 64.3 %all-gather.5.cloned.1.call-start = ((), (), s32[]{:S(2)}) async-start(), calls=%async_computation | async-start | bytes 1114112 | tf_op jit(solution)/shard_map/all_gather | solution.py:78
  9.4 4.5 %copy-start = (bf16[256,4096]{1,0:T(8,128)(2,1)S(1)}, bf16[256,4096]{1,0:T(8,128)(2,1)}, u32[]{:S(2)}) copy-start(bf16[256,4096]{1,0:T(8,128)(2,1)} %param.7) | copy-start | bytes 6291460
  30.4 73.6 %collective-permute-start.1 = (bf16[2,128,4096]{1,2,0:T(8,128)(2,1)}, bf16[2,128,4096]{1,2,0:T(8,128)(2,1)}, u32[]{:S(2)}, u32[]{:S(2)}) collective-permute-start(bf16[2,128,4096]{1,2,0:T(8,128)(2,1)} %pad_maximum_fusion.1), channel_id=1, source_target_pairs={{1,0},{2,1},{3,2},{4,3},{5,4},{6,5},{7,6},{8,7},{9,8},{10,9},{11,1... | collective-permute-start | bytes 6291464 | tf_op jit(solution)/shard_map/ppermute | solution.py:15
  38.1 89.2 %collective-permute-start = (bf16[2,128,4096]{1,2,0:T(8,128)(2,1)}, bf16[2,128,4096]{1,2,0:T(8,128)(2,1)}, u32[]{:S(2)}, u32[]{:S(2)}) collective-permute-start(bf16[2,128,4096]{1,2,0:T(8,128)(2,1)} %pad_maximum_fusion), channel_id=1, source_target_pairs={{0,1},{1,2},{2,3},{3,4},{4,5},{5,6},{6,7},{7,8},{8,9},{9,10},{10,1... | collective-permute-start | bytes 6291464 | tf_op jit(solution)/shard_map/ppermute | solution.py:15
  44.2 5.1 %copy-start.6 = (s32[2,32]{1,0:T(2,128)S(1)}, s32[2,32]{1,0:T(2,128)}, u32[]{:S(2)}) copy-start(s32[2,32]{1,0:T(2,128)} %param.9) | copy-start | bytes 772
  44.2 5.2 %copy-start.7 = (s32[2]{0:T(128)S(1)}, s32[2]{0:T(128)}, u32[]{:S(2)}) copy-start(s32[2]{0:T(128)} %param.8) | copy-start | bytes 28
  49.2 26.7 %copy-start.2 = (bf16[32,8,32,128]{3,2,1,0:T(8,128)(2,1)}, bf16[32,8,32,128]{3,2,1,0:T(8,128)(2,1)S(1)}, u32[]{:S(2)}) copy-start(bf16[32,8,32,128]{3,2,1,0:T(8,128)(2,1)S(1)} %copy.116) | copy-start | bytes 6291460
  135.9 4.0 %copy-start.3 = (f32[2,32,128,64]{2,3,0,1:T(8,128)S(1)}, f32[2,32,128,64]{2,3,0,1:T(8,128)}, u32[]{:S(2)}) copy-start(f32[2,32,128,64]{2,3,0,1:T(8,128)} %get-tuple-element.22) | copy-start | bytes 6291460
  135.9 4.6 %copy-start.4 = (bf16[8,32,8,128]{3,2,1,0:T(8,128)(2,1)S(1)}, bf16[8,32,8,128]{3,2,1,0:T(8,128)(2,1)}, u32[]{:S(2)}) copy-start(bf16[8,32,8,128]{3,2,1,0:T(8,128)(2,1)} %get-tuple-element.17) | copy-start | bytes 1572868
  139.9 1.6 %copy-start.1 = (bf16[1,256,32,128]{3,1,2,0:T(8,128)(2,1)S(1)}, bf16[1,256,32,128]{3,1,2,0:T(8,128)(2,1)}, u32[]{:S(2)}) copy-start(bf16[1,256,32,128]{3,1,2,0:T(8,128)(2,1)} %copy.96) | copy-start | bytes 6291460
  139.9 1.8 %copy-start.5 = (bf16[1,128,32,128]{3,1,2,0:T(8,128)(2,1)S(1)}, bf16[1,128,32,128]{3,1,2,0:T(8,128)(2,1)}, u32[]{:S(2)}) copy-start(bf16[1,128,32,128]{3,1,2,0:T(8,128)(2,1)} %copy.95) | copy-start | bytes 3145732
Sparse Core Ops, SparseCore 0:
  19.6 51.1 all-gather.4
